TPU v7x, 32 devices: a whole 2x2x4 slice. The times are simulated.
32 devices in a mesh: dp: 2 (over x), ty: 4 (over z), tx: 4 (over y, core).
Axes of the slice: x: 2, y: 2, z: 4, core: 2. Of those that a mesh axis runs over, the one named last changes fastest.
Arguments:
- x_in: bfloat16 [8, 512, 5120], P(('dp', 'ty'), None, 'tx'), parts along dimension 0
- w_q: bfloat16 [5120, 5120], P('tx', 'ty')
- w_k: bfloat16 [5120, 5120], P('tx', 'ty')
- w_v: bfloat16 [5120, 5120], P('tx', 'ty')
- w_o: bfloat16 [5120, 5120], P('ty', 'tx')
- w_gate: bfloat16 [5120, 13824], P('tx', 'ty')
- w_up: bfloat16 [5120, 13824], P('tx', 'ty')
- w_down: bfloat16 [13824, 5120], P('ty', 'tx')
Outputs:
- output: bfloat16 [8, 512, 5120], P(('dp', 'ty'), None, 'tx'), parts along dimension 0
There are 2 independent parts. A program takes and returns all parts, laid end to end along the dimension named above; an argument that names none is the same for every part.
All inputs are finite; a program needn't handle non-finite values.
Results may differ from a plain program's by a relative error of at most 0.0183301.
Values are sent between devices in bfloat16 or wider.
A program may use at most 1 GiB of HBM per device.

v0:
```python
import jax
import jax.numpy as jnp
import numpy as np
from jax import lax
from jax.experimental import pallas as pl
from jax.experimental.pallas import tpu as pltpu
from jax.sharding import PartitionSpec as P

HEAD_DIM = 128
EPS = 1e-5
THETA = 10000.0
BF = jnp.bfloat16
F32 = jnp.float32


def rot_tables(seq_len):
    half_dim = HEAD_DIM // 2
    inv_freq = np.float32(THETA) ** (-2.0 * np.arange(half_dim, dtype=np.float32) / np.float32(HEAD_DIM))
    angles = np.arange(seq_len, dtype=np.float32)[:, None] * inv_freq.astype(np.float32)[None, :]
    cos_t, sin_t = np.cos(angles), np.sin(angles)
    return np.concatenate([cos_t, cos_t], -1), np.concatenate([-sin_t, sin_t], -1)


def moments(vals):
    return jnp.stack([jnp.sum(vals, axis=-1), jnp.sum(vals * vals, axis=-1)], axis=-1)


def normed(vals, sums, full_width):
    mean_val = sums[..., 0:1] / full_width
    var_val = sums[..., 1:2] / full_width - mean_val * mean_val
    return ((vals - mean_val) * lax.rsqrt(var_val + EPS)).astype(BF)


MESH = pl.DeviceIdType.MESH
TILE = 384
VMEM_LIMIT = 67043328


def flip(index, by):
    low, high = index % 2, index // 2
    by_low, by_high = by % 2, by // 2
    return low + by_low - 2 * low * by_low + 2 * (high + by_high - 2 * high * by_high)


def greet(z, me):
    barrier = pltpu.get_barrier_semaphore()
    for by in (1, 2, 3):
        pl.semaphore_signal(barrier, inc=1, device_id={"ty": flip(z, by)}, device_id_type=MESH)
    pl.semaphore_signal(barrier, inc=1, device_id={"tx": flip(me, 1)}, device_id_type=MESH)
    pl.semaphore_signal(barrier, inc=1, device_id={"tx": flip(me, 2)}, device_id_type=MESH)
    pl.semaphore_wait(barrier, 5)


def remote(src, dst, send_sem, recv_sem, device_id):
    return pltpu.make_async_remote_copy(src_ref=src, dst_ref=dst, send_sem=send_sem, recv_sem=recv_sem, device_id=device_id, device_id_type=MESH)


def attn_kernel(n1_ref, x_ref, cos_ref, sin_ref, wq_hbm, wk_hbm, wv_hbm, wo_hbm, out_ref, xall, w_in, w_out, pbuf, r1, sbuf, r2, qbuf, kvbuf, abuf, zsend, zrecv, own,
                w_sem, own_sem, az_send, az_recv, p_send, p_recv, ry_send, ry_recv, kv_send, kv_recv, ay_send, ay_recv, ac_send, ac_recv, zr_send, zr_recv):
    z, me = lax.axis_index("ty"), lax.axis_index("tx")
    core, ypos = me % 2, me // 2
    core_peer, y_peer = {"tx": flip(me, 1)}, {"tx": flip(me, 2)}
    _, rows, width = n1_ref.shape
    half_cols = width // 2
    heads = half_cols // HEAD_DIM
    steps = 4
    inner = flip(z % 2, z // 2)

    def slot(i):
        turn = (i + 1) % 4
        return inner * ((4 - turn) % 4) + (1 - inner) * turn

    right_slot, left_slot = 1 + 2 * (z % 2), 3 - 2 * (z % 2)
    to_right = remote(n1_ref, xall.at[right_slot], az_send.at[0], az_recv.at[right_slot], {"ty": (z + 1) % 4})
    to_left = remote(n1_ref, xall.at[left_slot], az_send.at[1], az_recv.at[left_slot], {"ty": (z + 3) % 4})
    on_right = remote(xall.at[left_slot], xall.at[2], az_send.at[2], az_recv.at[2], {"ty": (z + 1) % 4})
    on_left = remote(xall.at[right_slot], xall.at[2], az_send.at[3], az_recv.at[2], {"ty": (z + 3) % 4})
    to_end = remote(xall.at[2], xall.at[3], az_send.at[4], az_recv.at[3], {"ty": (3 * z + 1) % 4})

    def arrived(by):
        remote(xall.at[by], xall.at[by], az_send.at[0], az_recv.at[by], {"ty": flip(z, 1)}).wait_recv()

    def core_copy(i):
        return remote(pbuf.at[1 - core], r1.at[i % 2], p_send.at[i % 2], p_recv.at[i % 2], core_peer)

    def y_copy(i):
        return remote(sbuf.at[i % 2, 1 - ypos], r2.at[i % 3], ry_send.at[i % 3], ry_recv.at[i % 3], y_peer)

    def kv_copy(i):
        piece = kvbuf.at[i % 2, core]
        return remote(piece, piece, kv_send.at[i % 2], kv_recv.at[i % 2], core_peer)

    def out_y_copy(i):
        piece = abuf.at[i % 3, core, ypos]
        return remote(piece, piece, ay_send.at[i % 3], ay_recv.at[i % 3], y_peer)

    def out_core_copy(i):
        piece = abuf.at[i % 3, core]
        return remote(piece, piece, ac_send.at[i % 3], ac_recv.at[i % 3], core_peer)

    def scatter_copy(i):
        by = slot(i)
        return remote(zsend.at[i % 2], zrecv.at[by - 1], zr_send.at[i % 2], zr_recv.at[by - 1], {"ty": flip(z, by)})

    loads = [pltpu.make_async_copy(w, w_in.at[n], w_sem.at[n]) for n, w in enumerate((wq_hbm, wk_hbm, wv_hbm))]
    loads.append(pltpu.make_async_copy(wo_hbm, w_out, w_sem.at[3]))
    own_copy = pltpu.make_async_copy(n1_ref, xall.at[0], own_sem)
    greet(z, me)

    @pl.when(z < 3)
    def _():
        to_right.start()

    @pl.when(z > 0)
    def _():
        to_left.start()

    own_copy.start()
    for load in loads:
        load.start()
    own_copy.wait()
    for load in loads:
        load.wait()

    @pl.when(z > 0)
    def _():
        arrived(left_slot)

    @pl.when((z > 0) & (z < 3))
    def _():
        on_right.start()

    @pl.when(z < 3)
    def _():
        arrived(right_slot)

    @pl.when((z > 0) & (z < 3))
    def _():
        on_left.start()

    def step(i, carry):
        @pl.when(i < steps)
        def _():
            by = slot(i)

            @pl.when(i == 1)
            def _():
                arrived(2)

                @pl.when((z > 0) & (z < 3))
                def _():
                    to_end.start()

            @pl.when((i == 2) & (z != 1) & (z != 2))
            def _():
                arrived(3)

            def product(t, carry):
                part = jnp.dot(xall[by, 1 - core], w_in[t], preferred_element_type=F32).astype(BF)
                pbuf[1 - core, 0, t] = part[:, :half_cols]
                pbuf[1 - core, 1, t] = part[:, half_cols:]
                return carry

            def near(t, carry):
                part = jnp.dot(xall[by, core], w_in[t], preferred_element_type=F32).astype(BF)
                pbuf[core, 0, t] = part[:, :half_cols]
                pbuf[core, 1, t] = part[:, half_cols:]
                return carry

            lax.fori_loop(0, 3, product, 0)
            core_copy(i).start()
            lax.fori_loop(0, 3, near, 0)
            core_copy(i).wait()

            def add(t, carry):
                for side in range(2):
                    sbuf[i % 2, side, t] = (pbuf[core, side, t].astype(F32) + r1[i % 2, side, t].astype(F32)).astype(BF)
                return carry

            lax.fori_loop(0, 3, add, 0)
            y_copy(i).start()

        @pl.when((i >= 1) & (i <= steps))
        def _():
            j = i - 1
            y_copy(j).wait()
            for h in range(heads):
                cols = slice(h * HEAD_DIM, (h + 1) * HEAD_DIM)

                def total(n):
                    return (sbuf[j % 2, ypos, n, :, cols].astype(F32) + r2[j % 3, n, :, cols].astype(F32)).astype(BF)

                def turned(vals):
                    vals = vals.astype(F32)
                    return (vals * cos_ref[core] + pltpu.roll(vals, HEAD_DIM // 2, 1) * sin_ref[core]).astype(BF)

                qbuf[:, cols] = turned(total(0))
                kvbuf[j % 2, core, 0, :, cols] = turned(total(1))
                kvbuf[j % 2, core, 1, :, cols] = total(2)
            kv_copy(j).start()
            kv_copy(j).wait()
            q_pos = core * rows + lax.broadcasted_iota(jnp.int32, (rows, 2 * rows), 0)
            allowed = q_pos >= lax.broadcasted_iota(jnp.int32, (rows, 2 * rows), 1)
            for h in range(heads):
                cols = slice(h * HEAD_DIM, (h + 1) * HEAD_DIM)
                keys = kvbuf[j % 2, :, 0, :, cols].reshape(2 * rows, HEAD_DIM)
                vals = kvbuf[j % 2, :, 1, :, cols].reshape(2 * rows, HEAD_DIM)
                scores = lax.dot_general(qbuf[:, cols], keys, (((1,), (1,)), ((), ())), preferred_element_type=F32) * HEAD_DIM ** -0.5
                scores = jnp.where(allowed, scores, -1e30)
                weight = jnp.exp(scores - jnp.max(scores, axis=1, keepdims=True))
                prob = (weight / jnp.sum(weight, axis=1, keepdims=True)).astype(BF)
                abuf[j % 3, core, ypos, :, cols] = jnp.dot(prob, vals, preferred_element_type=F32).astype(BF)
            out_y_copy(j).start()

        @pl.when(i >= 2)
        def _():
            j = i - 2
            by = slot(j)
            out_y_copy(j).wait()
            out_core_copy(j).start()

            @pl.when((j >= 2) & (j < steps - 1))
            def _():
                scatter_copy(j - 2).wait_send()

            out_core_copy(j).wait()

            def out(t, carry):
                cols = pl.ds(pl.multiple_of(t * 256, 256), 256)
                for half in range(2):
                    part = jnp.dot(abuf[j % 3, half, 0], w_out[0:half_cols, cols], preferred_element_type=F32)
                    part += jnp.dot(abuf[j % 3, half, 1], w_out[half_cols:, cols], preferred_element_type=F32)

                    @pl.when(by == 0)
                    def _():
                        own[half, :, cols] = part

                    @pl.when(by > 0)
                    def _():
                        zsend[j % 2, half, :, cols] = part.astype(BF)
                return carry

            lax.fori_loop(0, width // 256, out, 0)

            @pl.when(by > 0)
            def _():
                scatter_copy(j).start()
        return carry

    lax.fori_loop(0, steps + 2, step, 0)

    @pl.when(z < 3)
    def _():
        to_right.wait_send()

    @pl.when(z > 0)
    def _():
        to_left.wait_send()

    @pl.when((z > 0) & (z < 3))
    def _():
        on_right.wait_send()
        on_left.wait_send()
        to_end.wait_send()

    for j in (steps - 3, steps - 2):
        scatter_copy(j).wait_send()
    for by in (1, 2, 3):
        remote(zsend.at[0], zrecv.at[by - 1], zr_send.at[0], zr_recv.at[by - 1], {"ty": flip(z, by)}).wait_recv()

    def finish(t, carry):
        part = pl.ds(pl.multiple_of(t * 32, 32), 32)
        for half in range(2):
            total = own[half, part]
            for by in range(3):
                total += zrecv[by, half, part].astype(F32)
            out_ref[half, part] = (x_ref[half, part].astype(F32) + total.astype(BF).astype(F32)).astype(BF)
        return carry

    lax.fori_loop(0, rows // 32, finish, 0)


def attention(n1, x, w_q, w_k, w_v, w_o):
    seq_len, width = n1.shape
    rows, half_cols = seq_len // 2, width // 2
    cos_t, sin_t = rot_tables(seq_len)
    dma, vmem = pltpu.SemaphoreType.DMA, pltpu.VMEM
    in_vmem, anywhere = pl.BlockSpec(memory_space=pltpu.VMEM), pl.BlockSpec(memory_space=pl.ANY)
    out = pl.pallas_call(
        attn_kernel,
        name="attention",
        out_shape=jax.ShapeDtypeStruct((2, rows, width), BF),
        in_specs=[in_vmem] * 4 + [anywhere] * 4,
        out_specs=in_vmem,
        scratch_shapes=[
            vmem((4, 2, rows, width), BF),
            vmem((3, width, width), BF),
            vmem((width, width), BF),
            vmem((2, 2, 3, rows, half_cols), BF),
            vmem((2, 2, 3, rows, half_cols), BF),
            vmem((2, 2, 3, rows, half_cols), BF),
            vmem((3, 3, rows, half_cols), BF),
            vmem((rows, half_cols), BF),
            vmem((2, 2, 2, rows, half_cols), BF),
            vmem((3, 2, 2, rows, half_cols), BF),
            vmem((2, 2, rows, width), BF),
            vmem((3, 2, rows, width), BF),
            vmem((2, rows, width), F32),
            dma((4,)), dma, dma((5,)), dma((4,)),
            dma((2,)), dma((2,)), dma((3,)), dma((3,)), dma((2,)), dma((2,)),
            dma((3,)), dma((3,)), dma((3,)), dma((3,)),
            dma((2,)), dma((3,)),
        ],
        compiler_params=pltpu.CompilerParams(collective_id=1, has_side_effects=True, vmem_limit_bytes=VMEM_LIMIT),
    )(n1.reshape(2, rows, width), x.reshape(2, rows, width), jnp.asarray(cos_t).reshape(2, rows, HEAD_DIM), jnp.asarray(sin_t).reshape(2, rows, HEAD_DIM), w_q, w_k, w_v, w_o)
    return out.reshape(seq_len, width)


def mlp_kernel(n2_ref, h_ref, wg_hbm, wu_hbm, wd_hbm, out_ref, xall, w_in, w_out, pbuf, r1, sbuf, r2, abuf, zsend, zrecv, own,
               w_sem, own_sem, az_send, az_recv, p_send, p_recv, ry_send, ry_recv, ay_send, ay_recv, ac_send, ac_recv, zr_send, zr_recv):
    z, me = lax.axis_index("ty"), lax.axis_index("tx")
    core, ypos = me % 2, me // 2
    core_peer, y_peer = {"tx": flip(me, 1)}, {"tx": flip(me, 2)}
    halves, rows, width = n2_ref.shape
    ff = wg_hbm.shape[1]
    tiles = ff // TILE
    all_tiles = 2 * tiles
    quarter = rows // 4
    steps = 4 * halves

    def slot(i):
        return ((i + 1) // 2) % 4, (i + 1) % 2

    def gather_copy(by, half):
        return remote(n2_ref.at[half], xall.at[by, half], az_send.at[by, half], az_recv.at[by, half], {"ty": flip(z, by)})

    def core_copy(i, part):
        group = pl.ds(part * tiles, tiles)
        return remote(pbuf.at[1 - core, group], r1.at[i % 2, group], p_send.at[i % 2, part], p_recv.at[i % 2, part], core_peer)

    def y_copy(i, part):
        group = pl.ds(part * tiles, tiles)
        return remote(sbuf.at[i % 2, 1 - ypos, group], r2.at[i % 3, group], ry_send.at[i % 3, part], ry_recv.at[i % 3, part], y_peer)

    def act_y_copy(i):
        piece = abuf.at[i % 3, core, ypos]
        return remote(piece, piece, ay_send.at[i % 3], ay_recv.at[i % 3], y_peer)

    def act_core_copy(i):
        piece = abuf.at[i % 3, core]
        return remote(piece, piece, ac_send.at[i % 3], ac_recv.at[i % 3], core_peer)

    def scatter_copy(i):
        by, half = slot(i)
        return remote(zsend.at[i % 2], zrecv.at[by - 1, half], zr_send.at[i % 2], zr_recv.at[by - 1, half], {"ty": flip(z, by)})

    loads = [
        pltpu.make_async_copy(wg_hbm, w_in.at[:, pl.ds(0, ff)], w_sem.at[0]),
        pltpu.make_async_copy(wu_hbm, w_in.at[:, pl.ds(ff, ff)], w_sem.at[1]),
        pltpu.make_async_copy(wd_hbm, w_out, w_sem.at[2]),
    ]
    own_copy = pltpu.make_async_copy(n2_ref, xall.at[0], own_sem)
    own_copy.start()
    for load in loads:
        load.start()
    greet(z, me)
    for by in (1, 2, 3):
        for half in range(halves):
            gather_copy(by, half).start()
    own_copy.wait()
    loads[0].wait()
    loads[1].wait()

    def step(i, carry):
        @pl.when(i < steps)
        def _():
            by, half = slot(i)

            @pl.when((i > 0) & (i < steps - 1))
            def _():
                gather_copy(by, half).wait_recv()

            def product(t, carry):
                cols = pl.ds(pl.multiple_of(t * 2 * TILE, 2 * TILE), 2 * TILE)
                part = jnp.dot(xall[by, half], w_in[:, cols], preferred_element_type=F32).astype(BF)
                pbuf[:, 2 * t] = part[:, :TILE].reshape(2, 2, quarter, TILE)
                pbuf[:, 2 * t + 1] = part[:, TILE:].reshape(2, 2, quarter, TILE)
                return carry

            first = (tiles + 1) // 2
            lax.fori_loop(0, first, product, 0)
            core_copy(i, 0).start()
            lax.fori_loop(first, tiles, product, 0)
            core_copy(i, 1).start()
            for part in range(2):
                core_copy(i, part).wait_recv()

                def add(t, carry):
                    total = pbuf[core, t].astype(F32) + r1[i % 2, t].astype(F32)
                    total = total.astype(BF)
                    sbuf[i % 2, 0, t] = total[0]
                    sbuf[i % 2, 1, t] = total[1]
                    return carry

                lax.fori_loop(part * tiles, (part + 1) * tiles, add, 0)
                y_copy(i, part).start()
            for part in range(2):
                core_copy(i, part).wait_send()

        @pl.when((i >= 1) & (i <= steps))
        def _():
            j = i - 1
            for part in range(2):
                y_copy(j, part).wait()

            def gate(t, carry):
                g = (sbuf[j % 2, ypos, t].astype(F32) + r2[j % 3, t].astype(F32)).astype(BF).astype(F32)
                u = (sbuf[j % 2, ypos, tiles + t].astype(F32) + r2[j % 3, tiles + t].astype(F32)).astype(BF).astype(F32)
                cols = pl.ds(pl.multiple_of(t * TILE, TILE), TILE)
                abuf[j % 3, core, ypos, :, cols] = (g * jax.nn.sigmoid(g) * u).astype(BF)
                return carry

            lax.fori_loop(0, tiles, gate, 0)
            act_y_copy(j).start()

        @pl.when(i >= 2)
        def _():
            j = i - 2
            by, half = slot(j)
            act_y_copy(j).wait()
            act_core_copy(j).start()

            @pl.when(j == 0)
            def _():
                loads[2].wait()

            @pl.when((j >= 3) & (j < steps - 1))
            def _():
                scatter_copy(j - 2).wait_send()

            act_core_copy(j).wait()

            def down(t, carry):
                cols = pl.ds(pl.multiple_of(t * 256, 256), 256)
                part = jnp.dot(abuf[j % 3].reshape(rows, ff), w_out[:, cols], preferred_element_type=F32)

                @pl.when(by == 0)
                def _():
                    own[half, :, cols] = part

                @pl.when(by > 0)
                def _():
                    zsend[j % 2, :, cols] = part.astype(BF)
                return carry

            lax.fori_loop(0, width // 256, down, 0)

            @pl.when(by > 0)
            def _():
                scatter_copy(j).start()
        return carry

    lax.fori_loop(0, steps + 2, step, 0)

    for j in (steps - 3, steps - 2):
        scatter_copy(j).wait_send()
    for half in range(halves):
        for by in (1, 2, 3):
            gather_copy(by, half).wait_send()
            remote(zsend.at[0], zrecv.at[by - 1, half], zr_send.at[0], zr_recv.at[by - 1, half], {"ty": flip(z, by)}).wait_recv()

        def finish(t, carry):
            part = pl.ds(pl.multiple_of(t * 32, 32), 32)
            total = own[half, part]
            for by in range(3):
                total += zrecv[by, half, part].astype(F32)
            out_ref[half, part] = (h_ref[half, part].astype(F32) + total.astype(BF).astype(F32)).astype(BF)
            return carry

        lax.fori_loop(0, rows // 32, finish, 0)


def mlp(n2, h, w_gate, w_up, w_down):
    seq_len, width = n2.shape
    ff = w_gate.shape[1]
    halves = 2
    rows = seq_len // halves
    quarter = rows // 4
    tiles = ff // TILE
    dma, vmem = pltpu.SemaphoreType.DMA, pltpu.VMEM
    in_vmem, anywhere = pl.BlockSpec(memory_space=pltpu.VMEM), pl.BlockSpec(memory_space=pl.ANY)
    out = pl.pallas_call(
        mlp_kernel,
        name="mlp",
        out_shape=jax.ShapeDtypeStruct((halves, rows, width), BF),
        in_specs=[in_vmem, in_vmem, anywhere, anywhere, anywhere],
        out_specs=in_vmem,
        scratch_shapes=[
            vmem((4, halves, rows, width), BF),
            vmem((width, 2 * ff), BF),
            vmem((ff, width), BF),
            vmem((2, 2 * tiles, 2, quarter, TILE), BF),
            vmem((2, 2 * tiles, 2, quarter, TILE), BF),
            vmem((2, 2, 2 * tiles, quarter, TILE), BF),
            vmem((3, 2 * tiles, quarter, TILE), BF),
            vmem((3, 2, 2, quarter, ff), BF),
            vmem((2, rows, width), BF),
            vmem((3, halves, rows, width), BF),
            vmem((halves, rows, width), F32),
            dma((3,)), dma, dma((4, halves)), dma((4, halves)),
            dma((2, 2)), dma((2, 2)), dma((3, 2)), dma((3, 2)),
            dma((3,)), dma((3,)), dma((3,)), dma((3,)),
            dma((2,)), dma((3, halves)),
        ],
        compiler_params=pltpu.CompilerParams(collective_id=0, has_side_effects=True, vmem_limit_bytes=VMEM_LIMIT),
    )(n2.reshape(halves, rows, width), h.reshape(halves, rows, width), w_gate, w_up, w_down)
    return out.reshape(seq_len, width)


def solution(mesh):
    tx_count = mesh.shape["tx"]
    act_spec = P(("dp", "ty"), None, "tx")
    col_spec = P("tx", "ty")
    row_spec = P("ty", "tx")

    def layer_fn(x_blk, w_q, w_k, w_v, w_o, w_gate, w_up, w_down):
        full_width = x_blk.shape[-1] * tx_count

        def norm(vals):
            vals = vals.astype(F32)
            return normed(vals, lax.psum(moments(vals), "tx"), full_width)

        x = x_blk[0]
        h = attention(norm(x), x, w_q, w_k, w_v, w_o)
        return mlp(norm(h), h, w_gate, w_up, w_down)[None]

    return jax.shard_map(layer_fn, mesh=mesh, in_specs=(act_spec, col_spec, col_spec, col_spec, row_spec, col_spec, col_spec, row_spec), out_specs=act_spec, check_vma=False)
```

profile of v0, /device:TPU:0, one launch (start us, length us, event | category | flops | bytes accessed | tf_op | source)
XLA Modules:
  0.0 555.9 jit_solution(164234769377970184)
XLA Ops:
  0.0 1.8 convert_reduce_fusion.1
  1.8 8.4 %psum.14 = f32[512,2]{0,1:T(2,128)S(1)} all-reduce(f32[512,2]{0,1:T(2,128)S(1)} %pad_maximum_fusion), channel_id=1, replica_groups=mesh['dp'=2,'ty'=4,'tx'=4] {'tx'}, use_global_device_ids=true, to_apply=%region_2.0 | all-reduce | flops 1024 | bytes 8192 | tf_op jit(solution)/shard_map/psum | solution.py:531
  10.3 2.7 multiply_convert_fusion.n1_ref
  13.1 251.3 %attention.1.h_ref = bf16[2,256,1280]{2,1,0:T(8,128)(2,1)} custom-call(bf16[2,256,1280]{2,1,0:T(8,128)(2,1)} %multiply_convert_fusion.n1_ref, bf16[2,256,1280]{2,1,0:T(8,128)(2,1)} %bitcast.13, f32[2,256,128]{2,1,0:T(8,128)} %constant.17.cos_ref, f32[2,256,128]{2,1,0:T(8,128)} %constant.18.sin_ref, bf16[1280,1280]{1,0:T(8,128)(2,1)} %wq_hbm.1, ...), custom_call_target="tpu_custom_call" | custom-call | tf_op jit(solution)/shard_map/attention/pallas_call | solution.py:289
  264.4 1.8 convert_reduce_fusion
  266.2 5.8 %psum.15 = f32[512,2]{0,1:T(2,128)S(1)} all-reduce(f32[512,2]{0,1:T(2,128)S(1)} %pad_maximum_fusion.1), channel_id=1, replica_groups=mesh['dp'=2,'ty'=4,'tx'=4] {'tx'}, use_global_device_ids=true, to_apply=%region_5.0 | all-reduce | flops 1024 | bytes 8192 | tf_op jit(solution)/shard_map/psum | solution.py:531
  272.0 2.7 fusion.3.n2_ref
  274.8 278.6 %mlp.1 = bf16[2,256,1280]{2,1,0:T(8,128)(2,1)} custom-call(bf16[2,256,1280]{2,1,0:T(8,128)(2,1)} %fusion.3.n2_ref, bf16[2,256,1280]{2,1,0:T(8,128)(2,1)} %attention.1.h_ref, bf16[1280,3456]{1,0:T(8,128)(2,1)} %wg_hbm.1, bf16[1280,3456]{1,0:T(8,128)(2,1)} %wu_hbm.1, bf16[3456,1280]{1,0:T(8,128)(2,1)} %wd_hbm.1), custom_call_target="tpu_custom_call" | custom-call | tf_op jit(solution)/shard_map/mlp/pallas_call | solution.py:492
  553.4 2.5 copy.14
  (10 shorter events, 0.2 us)
where the time goes:
time: 556 us
  Pallas kernels  530 us (95%)
  blocking collectives  14.2 us (3%)
  other arithmetic  9.15 us (2%)
    pallas_call x1, Pallas kernels, mlp(): pl.pallas_call(mlp_kernel, name='mlp', out_shape=jax.ShapeDtypeStruct((ha...  279 us
    pallas_call x1, Pallas kernels, attention(): pl.pallas_call(attn_kernel, name='attention', out_shape=jax.ShapeDtypeStr...  251 us
    psum x2, blocking collectives, norm(): return normed(vals, lax.psum(moments(vals), 'tx'), full_width)  14.2 us

commit v1 on v0

--- a/solution.py
+++ b/solution.py
@@ -21,16 +21,6 @@
     return np.concatenate([cos_t, cos_t], -1), np.concatenate([-sin_t, sin_t], -1)
 
 
-def moments(vals):
-    return jnp.stack([jnp.sum(vals, axis=-1), jnp.sum(vals * vals, axis=-1)], axis=-1)
-
-
-def normed(vals, sums, full_width):
-    mean_val = sums[..., 0:1] / full_width
-    var_val = sums[..., 1:2] / full_width - mean_val * mean_val
-    return ((vals - mean_val) * lax.rsqrt(var_val + EPS)).astype(BF)
-
-
 MESH = pl.DeviceIdType.MESH
 TILE = 384
 VMEM_LIMIT = 67043328
@@ -51,28 +41,53 @@
     pl.semaphore_wait(barrier, 5)
 
 
+def norm_rows(src, dst, stats, send_sem, recv_sem, core_peer, y_peer):
+    halves, rows, width = src.shape
+    total_rows = halves * rows
+    full_width = 4 * width
+    lane = lax.broadcasted_iota(jnp.int32, (rows, 128), 1)
+    for half in range(halves):
+        vals = src[half].astype(F32)
+        both = jnp.where(lane == 0, jnp.sum(vals, axis=1, keepdims=True), jnp.sum(vals * vals, axis=1, keepdims=True))
+        stats[0, :, half * rows:(half + 1) * rows] = both.T[:8]
+    swap = remote(stats.at[0], stats.at[1], send_sem.at[0], recv_sem.at[0], core_peer)
+    swap.start()
+    swap.wait()
+    stats[2] = stats[0] + stats[1]
+    swap = remote(stats.at[2], stats.at[3], send_sem.at[1], recv_sem.at[1], y_peer)
+    swap.start()
+    swap.wait()
+    sums = stats[2] + stats[3]
+    sums = jnp.concatenate([sums, jnp.zeros((120, total_rows), F32)], 0).T
+    mean_val = sums[:, 0:1] / full_width
+    var_val = sums[:, 1:2] / full_width - mean_val * mean_val
+    scale = lax.rsqrt(var_val + EPS)
+    for half in range(halves):
+        part = slice(half * rows, (half + 1) * rows)
+        dst[half] = ((src[half].astype(F32) - mean_val[part]) * scale[part]).astype(BF)
+
+
 def remote(src, dst, send_sem, recv_sem, device_id):
     return pltpu.make_async_remote_copy(src_ref=src, dst_ref=dst, send_sem=send_sem, recv_sem=recv_sem, device_id=device_id, device_id_type=MESH)
 
 
-def attn_kernel(n1_ref, x_ref, cos_ref, sin_ref, wq_hbm, wk_hbm, wv_hbm, wo_hbm, out_ref, xall, w_in, w_out, pbuf, r1, sbuf, r2, qbuf, kvbuf, abuf, zsend, zrecv, own,
-                w_sem, own_sem, az_send, az_recv, p_send, p_recv, ry_send, ry_recv, kv_send, kv_recv, ay_send, ay_recv, ac_send, ac_recv, zr_send, zr_recv):
+def attn_kernel(x_ref, cos_ref, sin_ref, wq_hbm, wk_hbm, wv_hbm, wo_hbm, out_ref, xall, w_in, w_out, pbuf, r1, sbuf, r2, qbuf, kvbuf, abuf, zsend, zrecv, own,
+                stats, s_send, s_recv, w_sem, az_send, az_recv, p_send, p_recv, ry_send, ry_recv, kv_send, kv_recv, ay_send, ay_recv, ac_send, ac_recv, zr_send, zr_recv):
     z, me = lax.axis_index("ty"), lax.axis_index("tx")
     core, ypos = me % 2, me // 2
     core_peer, y_peer = {"tx": flip(me, 1)}, {"tx": flip(me, 2)}
-    _, rows, width = n1_ref.shape
+    _, rows, width = x_ref.shape
     half_cols = width // 2
     heads = half_cols // HEAD_DIM
     steps = 4
     inner = flip(z % 2, z // 2)
 
     def slot(i):
-        turn = (i + 1) % 4
-        return inner * ((4 - turn) % 4) + (1 - inner) * turn
+        return inner * ((4 - i) % 4) + (1 - inner) * (i % 4)
 
     right_slot, left_slot = 1 + 2 * (z % 2), 3 - 2 * (z % 2)
-    to_right = remote(n1_ref, xall.at[right_slot], az_send.at[0], az_recv.at[right_slot], {"ty": (z + 1) % 4})
-    to_left = remote(n1_ref, xall.at[left_slot], az_send.at[1], az_recv.at[left_slot], {"ty": (z + 3) % 4})
+    to_right = remote(xall.at[0], xall.at[right_slot], az_send.at[0], az_recv.at[right_slot], {"ty": (z + 1) % 4})
+    to_left = remote(xall.at[0], xall.at[left_slot], az_send.at[1], az_recv.at[left_slot], {"ty": (z + 3) % 4})
     on_right = remote(xall.at[left_slot], xall.at[2], az_send.at[2], az_recv.at[2], {"ty": (z + 1) % 4})
     on_left = remote(xall.at[right_slot], xall.at[2], az_send.at[3], az_recv.at[2], {"ty": (z + 3) % 4})
     to_end = remote(xall.at[2], xall.at[3], az_send.at[4], az_recv.at[3], {"ty": (3 * z + 1) % 4})
@@ -98,14 +113,16 @@
         piece = abuf.at[i % 3, core]
         return remote(piece, piece, ac_send.at[i % 3], ac_recv.at[i % 3], core_peer)
 
-    def scatter_copy(i):
+    def scatter_copy(i, half):
         by = slot(i)
-        return remote(zsend.at[i % 2], zrecv.at[by - 1], zr_send.at[i % 2], zr_recv.at[by - 1], {"ty": flip(z, by)})
+        return remote(zsend.at[i % 2, half], zrecv.at[by - 1, half], zr_send.at[i % 2, half], zr_recv.at[by - 1, half], {"ty": flip(z, by)})
 
     loads = [pltpu.make_async_copy(w, w_in.at[n], w_sem.at[n]) for n, w in enumerate((wq_hbm, wk_hbm, wv_hbm))]
     loads.append(pltpu.make_async_copy(wo_hbm, w_out, w_sem.at[3]))
-    own_copy = pltpu.make_async_copy(n1_ref, xall.at[0], own_sem)
+    for load in loads:
+        load.start()
     greet(z, me)
+    norm_rows(x_ref, xall.at[0], stats, s_send, s_recv, core_peer, y_peer)
 
     @pl.when(z < 3)
     def _():
@@ -115,43 +132,39 @@
     def _():
         to_left.start()
 
-    own_copy.start()
-    for load in loads:
-        load.start()
-    own_copy.wait()
     for load in loads:
         load.wait()
-
-    @pl.when(z > 0)
-    def _():
-        arrived(left_slot)
-
-    @pl.when((z > 0) & (z < 3))
-    def _():
-        on_right.start()
-
-    @pl.when(z < 3)
-    def _():
-        arrived(right_slot)
-
-    @pl.when((z > 0) & (z < 3))
-    def _():
-        on_left.start()
 
     def step(i, carry):
         @pl.when(i < steps)
         def _():
             by = slot(i)
 
-            @pl.when(i == 1)
+            @pl.when((i == 1) & (z > 0))
+            def _():
+                arrived(left_slot)
+
+            @pl.when((i == 1) & (z > 0) & (z < 3))
+            def _():
+                on_right.start()
+
+            @pl.when((i == 1) & (z < 3))
+            def _():
+                arrived(right_slot)
+
+            @pl.when((i == 1) & (z > 0) & (z < 3))
+            def _():
+                on_left.start()
+
+            @pl.when(i == 2)
             def _():
                 arrived(2)
 
-                @pl.when((z > 0) & (z < 3))
-                def _():
-                    to_end.start()
-
-            @pl.when((i == 2) & (z != 1) & (z != 2))
+            @pl.when((i == 2) & (z > 0) & (z < 3))
+            def _():
+                to_end.start()
+
+            @pl.when((i == 3) & (z != 1) & (z != 2))
             def _():
                 arrived(3)
 
@@ -215,36 +228,39 @@
         @pl.when(i >= 2)
         def _():
             j = i - 2
-            by = slot(j)
             out_y_copy(j).wait()
             out_core_copy(j).start()
 
-            @pl.when((j >= 2) & (j < steps - 1))
-            def _():
-                scatter_copy(j - 2).wait_send()
+            @pl.when(j >= 3)
+            def _():
+                scatter_copy(j - 2, 0).wait_send()
+                scatter_copy(j - 2, 1).wait_send()
 
             out_core_copy(j).wait()
 
-            def out(t, carry):
-                cols = pl.ds(pl.multiple_of(t * 256, 256), 256)
-                for half in range(2):
+            def out_half(half, carry):
+                def out(t, carry):
+                    cols = pl.ds(pl.multiple_of(t * 256, 256), 256)
                     part = jnp.dot(abuf[j % 3, half, 0], w_out[0:half_cols, cols], preferred_element_type=F32)
                     part += jnp.dot(abuf[j % 3, half, 1], w_out[half_cols:, cols], preferred_element_type=F32)
 
-                    @pl.when(by == 0)
+                    @pl.when(j == 0)
                     def _():
                         own[half, :, cols] = part
 
-                    @pl.when(by > 0)
+                    @pl.when(j > 0)
                     def _():
                         zsend[j % 2, half, :, cols] = part.astype(BF)
-                return carry
-
-            lax.fori_loop(0, width // 256, out, 0)
-
-            @pl.when(by > 0)
-            def _():
-                scatter_copy(j).start()
+                    return carry
+
+                lax.fori_loop(0, width // 256, out, 0)
+
+                @pl.when(j > 0)
+                def _():
+                    scatter_copy(j, half).start()
+                return carry
+
+            lax.fori_loop(0, 2, out_half, 0)
         return carry
 
     lax.fori_loop(0, steps + 2, step, 0)
@@ -263,25 +279,25 @@
         on_left.wait_send()
         to_end.wait_send()
 
-    for j in (steps - 3, steps - 2):
-        scatter_copy(j).wait_send()
-    for by in (1, 2, 3):
-        remote(zsend.at[0], zrecv.at[by - 1], zr_send.at[0], zr_recv.at[by - 1], {"ty": flip(z, by)}).wait_recv()
-
-    def finish(t, carry):
-        part = pl.ds(pl.multiple_of(t * 32, 32), 32)
-        for half in range(2):
+    for half in range(2):
+        for j in (steps - 2, steps - 1):
+            scatter_copy(j, half).wait_send()
+        for by in (1, 2, 3):
+            remote(zsend.at[0, half], zrecv.at[by - 1, half], zr_send.at[0, half], zr_recv.at[by - 1, half], {"ty": flip(z, by)}).wait_recv()
+
+        def finish(t, carry):
+            part = pl.ds(pl.multiple_of(t * 32, 32), 32)
             total = own[half, part]
             for by in range(3):
                 total += zrecv[by, half, part].astype(F32)
             out_ref[half, part] = (x_ref[half, part].astype(F32) + total.astype(BF).astype(F32)).astype(BF)
-        return carry
-
-    lax.fori_loop(0, rows // 32, finish, 0)
-
-
-def attention(n1, x, w_q, w_k, w_v, w_o):
-    seq_len, width = n1.shape
+            return carry
+
+        lax.fori_loop(0, rows // 32, finish, 0)
+
+
+def attention(x, w_q, w_k, w_v, w_o):
+    seq_len, width = x.shape
     rows, half_cols = seq_len // 2, width // 2
     cos_t, sin_t = rot_tables(seq_len)
     dma, vmem = pltpu.SemaphoreType.DMA, pltpu.VMEM
@@ -290,7 +306,7 @@
         attn_kernel,
         name="attention",
         out_shape=jax.ShapeDtypeStruct((2, rows, width), BF),
-        in_specs=[in_vmem] * 4 + [anywhere] * 4,
+        in_specs=[in_vmem] * 3 + [anywhere] * 4,
         out_specs=in_vmem,
         scratch_shapes=[
             vmem((4, 2, rows, width), BF),
@@ -306,22 +322,23 @@
             vmem((2, 2, rows, width), BF),
             vmem((3, 2, rows, width), BF),
             vmem((2, rows, width), F32),
-            dma((4,)), dma, dma((5,)), dma((4,)),
+            vmem((4, 8, seq_len), F32), dma((2,)), dma((2,)),
+            dma((4,)), dma((5,)), dma((4,)),
             dma((2,)), dma((2,)), dma((3,)), dma((3,)), dma((2,)), dma((2,)),
             dma((3,)), dma((3,)), dma((3,)), dma((3,)),
-            dma((2,)), dma((3,)),
+            dma((2, 2)), dma((3, 2)),
         ],
         compiler_params=pltpu.CompilerParams(collective_id=1, has_side_effects=True, vmem_limit_bytes=VMEM_LIMIT),
-    )(n1.reshape(2, rows, width), x.reshape(2, rows, width), jnp.asarray(cos_t).reshape(2, rows, HEAD_DIM), jnp.asarray(sin_t).reshape(2, rows, HEAD_DIM), w_q, w_k, w_v, w_o)
+    )(x.reshape(2, rows, width), jnp.asarray(cos_t).reshape(2, rows, HEAD_DIM), jnp.asarray(sin_t).reshape(2, rows, HEAD_DIM), w_q, w_k, w_v, w_o)
     return out.reshape(seq_len, width)
 
 
-def mlp_kernel(n2_ref, h_ref, wg_hbm, wu_hbm, wd_hbm, out_ref, xall, w_in, w_out, pbuf, r1, sbuf, r2, abuf, zsend, zrecv, own,
-               w_sem, own_sem, az_send, az_recv, p_send, p_recv, ry_send, ry_recv, ay_send, ay_recv, ac_send, ac_recv, zr_send, zr_recv):
+def mlp_kernel(h_ref, wg_hbm, wu_hbm, wd_hbm, out_ref, xall, w_in, w_out, pbuf, r1, sbuf, r2, abuf, zsend, zrecv, own,
+               stats, s_send, s_recv, w_sem, az_send, az_recv, p_send, p_recv, ry_send, ry_recv, ay_send, ay_recv, ac_send, ac_recv, zr_send, zr_recv):
     z, me = lax.axis_index("ty"), lax.axis_index("tx")
     core, ypos = me % 2, me // 2
     core_peer, y_peer = {"tx": flip(me, 1)}, {"tx": flip(me, 2)}
-    halves, rows, width = n2_ref.shape
+    halves, rows, width = h_ref.shape
     ff = wg_hbm.shape[1]
     tiles = ff // TILE
     all_tiles = 2 * tiles
@@ -332,7 +349,7 @@
         return ((i + 1) // 2) % 4, (i + 1) % 2
 
     def gather_copy(by, half):
-        return remote(n2_ref.at[half], xall.at[by, half], az_send.at[by, half], az_recv.at[by, half], {"ty": flip(z, by)})
+        return remote(xall.at[0, half], xall.at[by, half], az_send.at[by, half], az_recv.at[by, half], {"ty": flip(z, by)})
 
     def core_copy(i, part):
         group = pl.ds(part * tiles, tiles)
@@ -359,15 +376,13 @@
         pltpu.make_async_copy(wu_hbm, w_in.at[:, pl.ds(ff, ff)], w_sem.at[1]),
         pltpu.make_async_copy(wd_hbm, w_out, w_sem.at[2]),
     ]
-    own_copy = pltpu.make_async_copy(n2_ref, xall.at[0], own_sem)
-    own_copy.start()
     for load in loads:
         load.start()
     greet(z, me)
+    norm_rows(h_ref, xall.at[0], stats, s_send, s_recv, core_peer, y_peer)
     for by in (1, 2, 3):
         for half in range(halves):
             gather_copy(by, half).start()
-    own_copy.wait()
     loads[0].wait()
     loads[1].wait()
 
@@ -480,8 +495,8 @@
         lax.fori_loop(0, rows // 32, finish, 0)
 
 
-def mlp(n2, h, w_gate, w_up, w_down):
-    seq_len, width = n2.shape
+def mlp(h, w_gate, w_up, w_down):
+    seq_len, width = h.shape
     ff = w_gate.shape[1]
     halves = 2
     rows = seq_len // halves
@@ -493,7 +508,7 @@
         mlp_kernel,
         name="mlp",
         out_shape=jax.ShapeDtypeStruct((halves, rows, width), BF),
-        in_specs=[in_vmem, in_vmem, anywhere, anywhere, anywhere],
+        in_specs=[in_vmem, anywhere, anywhere, anywhere],
         out_specs=in_vmem,
         scratch_shapes=[
             vmem((4, halves, rows, width), BF),
@@ -507,31 +522,24 @@
             vmem((2, rows, width), BF),
             vmem((3, halves, rows, width), BF),
             vmem((halves, rows, width), F32),
-            dma((3,)), dma, dma((4, halves)), dma((4, halves)),
+            vmem((4, 8, seq_len), F32), dma((2,)), dma((2,)),
+            dma((3,)), dma((4, halves)), dma((4, halves)),
             dma((2, 2)), dma((2, 2)), dma((3, 2)), dma((3, 2)),
             dma((3,)), dma((3,)), dma((3,)), dma((3,)),
             dma((2,)), dma((3, halves)),
         ],
         compiler_params=pltpu.CompilerParams(collective_id=0, has_side_effects=True, vmem_limit_bytes=VMEM_LIMIT),
-    )(n2.reshape(halves, rows, width), h.reshape(halves, rows, width), w_gate, w_up, w_down)
+    )(h.reshape(halves, rows, width), w_gate, w_up, w_down)
     return out.reshape(seq_len, width)
 
 
 def solution(mesh):
-    tx_count = mesh.shape["tx"]
     act_spec = P(("dp", "ty"), None, "tx")
     col_spec = P("tx", "ty")
     row_spec = P("ty", "tx")
 
     def layer_fn(x_blk, w_q, w_k, w_v, w_o, w_gate, w_up, w_down):
-        full_width = x_blk.shape[-1] * tx_count
-
-        def norm(vals):
-            vals = vals.astype(F32)
-            return normed(vals, lax.psum(moments(vals), "tx"), full_width)
-
-        x = x_blk[0]
-        h = attention(norm(x), x, w_q, w_k, w_v, w_o)
-        return mlp(norm(h), h, w_gate, w_up, w_down)[None]
+        h = attention(x_blk[0], w_q, w_k, w_v, w_o)
+        return mlp(h, w_gate, w_up, w_down)[None]
 
     return jax.shard_map(layer_fn, mesh=mesh, in_specs=(act_spec, col_spec, col_spec, col_spec, row_spec, col_spec, col_spec, row_spec), out_specs=act_spec, check_vma=False)

time: 556 us -> 518 us (0.932)
  Pallas kernels: 530 us -> 515 us
  blocking collectives: 14.2 us -> 0 us
  other arithmetic: 9.15 us -> 0 us
    pallas_call x1, Pallas kernels: 251 us -> 231 us  [attention(): pl.pallas_call(attn_kernel, name='attention', out_shape=jax.ShapeDtypeStr...]
    psum x2 -> x0, blocking collectives: 14.2 us -> none  [norm(): return normed(vals, lax.psum(moments(vals), 'tx'), full_width)]
where the time goes in v1:
time: 518 us
  Pallas kernels  515 us (99%)
    pallas_call x1, Pallas kernels, mlp(): pl.pallas_call(mlp_kernel, name='mlp', out_shape=jax.ShapeDtypeStruct((ha...  284 us
    pallas_call x1, Pallas kernels, attention(): pl.pallas_call(attn_kernel, name='attention', out_shape=jax.ShapeDtypeStr...  231 us

profile of v1, /device:TPU:0, one launch (start us, length us, event | category | flops | bytes accessed | tf_op | source)
XLA Modules:
  0.0 517.8 jit_solution(8291413827772550197)
XLA Ops:
  0.0 231.3 %attention.1.h_ref = bf16[2,256,1280]{2,1,0:T(8,128)(2,1)} custom-call(bf16[2,256,1280]{2,1,0:T(8,128)(2,1)} %bitcast.3, f32[2,256,128]{2,1,0:T(8,128)} %constant.7.cos_ref, f32[2,256,128]{2,1,0:T(8,128)} %constant.8.sin_ref, bf16[1280,1280]{1,0:T(8,128)(2,1)} %wq_hbm.1, bf16[1280,1280]{1,0:T(8,128)(2,1)} %wk_hbm.1, bf16[1280,1280]{1,0:T(8,128)(2,1)} %wv_hbm.1, ...), custom_call_target="tpu_custom_call" | custom-call | tf_op jit(solution)/shard_map/attention/pallas_call | solution.py:305
  231.3 284.0 %mlp.1 = bf16[2,256,1280]{2,1,0:T(8,128)(2,1)} custom-call(bf16[2,256,1280]{2,1,0:T(8,128)(2,1)} %attention.1.h_ref, bf16[1280,3456]{1,0:T(8,128)(2,1)} %wg_hbm.1, bf16[1280,3456]{1,0:T(8,128)(2,1)} %wu_hbm.1, bf16[3456,1280]{1,0:T(8,128)(2,1)} %wd_hbm.1), custom_call_target="tpu_custom_call" | custom-call | tf_op jit(solution)/shard_map/mlp/pallas_call | solution.py:507
  515.3 2.5 copy.12

commit v2 on v1

v2 whole, which is shorter than its diff:
```python
import jax
import jax.numpy as jnp
import numpy as np
from jax import lax
from jax.experimental import pallas as pl
from jax.experimental.pallas import tpu as pltpu
from jax.sharding import PartitionSpec as P

HEAD_DIM = 128
EPS = 1e-5
THETA = 10000.0
BF = jnp.bfloat16
F32 = jnp.float32


def rot_tables(seq_len):
    half_dim = HEAD_DIM // 2
    inv_freq = np.float32(THETA) ** (-2.0 * np.arange(half_dim, dtype=np.float32) / np.float32(HEAD_DIM))
    angles = np.arange(seq_len, dtype=np.float32)[:, None] * inv_freq.astype(np.float32)[None, :]
    cos_t, sin_t = np.cos(angles), np.sin(angles)
    return np.concatenate([cos_t, cos_t], -1), np.concatenate([-sin_t, sin_t], -1)


MESH = pl.DeviceIdType.MESH
TILE = 384
VMEM_LIMIT = 67043328


def flip(index, by):
    low, high = index % 2, index // 2
    by_low, by_high = by % 2, by // 2
    return low + by_low - 2 * low * by_low + 2 * (high + by_high - 2 * high * by_high)


def greet(z, me):
    barrier = pltpu.get_barrier_semaphore()
    for by in (1, 2, 3):
        pl.semaphore_signal(barrier, inc=1, device_id={"ty": flip(z, by)}, device_id_type=MESH)
    pl.semaphore_signal(barrier, inc=1, device_id={"tx": flip(me, 1)}, device_id_type=MESH)
    pl.semaphore_signal(barrier, inc=1, device_id={"tx": flip(me, 2)}, device_id_type=MESH)
    pl.semaphore_wait(barrier, 5)


def norm_rows(src, dst, stats, send_sem, recv_sem, core_peer, y_peer, ready):
    halves, rows, width = src.shape
    total_rows = halves * rows
    full_width = 4 * width
    lane = lax.broadcasted_iota(jnp.int32, (rows, 128), 1)
    for half in range(halves):
        vals = src[half].astype(F32)
        both = jnp.where(lane == 0, jnp.sum(vals, axis=1, keepdims=True), jnp.sum(vals * vals, axis=1, keepdims=True))
        stats[0, :, half * rows:(half + 1) * rows] = both.T[:8]
    swap = remote(stats.at[0], stats.at[1], send_sem.at[0], recv_sem.at[0], core_peer)
    swap.start()
    swap.wait()
    stats[2] = stats[0] + stats[1]
    swap = remote(stats.at[2], stats.at[3], send_sem.at[1], recv_sem.at[1], y_peer)
    swap.start()
    swap.wait()
    sums = stats[2] + stats[3]
    sums = jnp.concatenate([sums, jnp.zeros((120, total_rows), F32)], 0).T
    mean_val = sums[:, 0:1] / full_width
    var_val = sums[:, 1:2] / full_width - mean_val * mean_val
    scale = lax.rsqrt(var_val + EPS)
    for half in range(halves):
        part = slice(half * rows, (half + 1) * rows)
        dst[half] = ((src[half].astype(F32) - mean_val[part]) * scale[part]).astype(BF)
        ready(half)


def remote(src, dst, send_sem, recv_sem, device_id):
    return pltpu.make_async_remote_copy(src_ref=src, dst_ref=dst, send_sem=send_sem, recv_sem=recv_sem, device_id=device_id, device_id_type=MESH)


def attn_kernel(x_ref, cos_ref, sin_ref, wq_hbm, wk_hbm, wv_hbm, wo_hbm, out_ref, xall, w_in, w_out, pbuf, r1, sbuf, r2, qbuf, kvbuf, abuf, zsend, zrecv, own,
                stats, s_send, s_recv, w_sem, az_send, az_recv, p_send, p_recv, ry_send, ry_recv, kv_send, kv_recv, ay_send, ay_recv, ac_send, ac_recv, zr_send, zr_recv):
    z, me = lax.axis_index("ty"), lax.axis_index("tx")
    core, ypos = me % 2, me // 2
    core_peer, y_peer = {"tx": flip(me, 1)}, {"tx": flip(me, 2)}
    halves, rows, width = x_ref.shape
    piece_rows = rows // 2
    half_cols = width // 2
    heads = half_cols // HEAD_DIM
    steps = 4 * halves
    inner = flip(z % 2, z // 2)

    def slot(i):
        turn = ((i + 1) // 2) % 4
        edge = 1 - (i * (steps - 1 - i) + 11) // 12
        return inner * ((4 - turn) % 4) + (1 - inner) * turn, (i + 1 + edge) % 2

    right_slot, left_slot = 1 + 2 * (z % 2), 3 - 2 * (z % 2)

    def to_right(half):
        return remote(xall.at[0, half], xall.at[right_slot, half], az_send.at[0, half], az_recv.at[right_slot, half], {"ty": (z + 1) % 4})

    def to_left(half):
        return remote(xall.at[0, half], xall.at[left_slot, half], az_send.at[1, half], az_recv.at[left_slot, half], {"ty": (z + 3) % 4})

    def on_right(half):
        return remote(xall.at[left_slot, half], xall.at[2, half], az_send.at[2, half], az_recv.at[2, half], {"ty": (z + 1) % 4})

    def on_left(half):
        return remote(xall.at[right_slot, half], xall.at[2, half], az_send.at[3, half], az_recv.at[2, half], {"ty": (z + 3) % 4})

    def to_end(half):
        return remote(xall.at[2, half], xall.at[3, half], az_send.at[4, half], az_recv.at[3, half], {"ty": (3 * z + 1) % 4})

    def arrived(by, half):
        remote(xall.at[by, half], xall.at[by, half], az_send.at[0, half], az_recv.at[by, half], {"ty": flip(z, 1)}).wait_recv()

    def core_copy(i):
        return remote(pbuf.at[1 - core], r1.at[i % 2], p_send.at[i % 2], p_recv.at[i % 2], core_peer)

    def y_copy(i):
        return remote(sbuf.at[i % 2, 1 - ypos], r2.at[i % 3], ry_send.at[i % 3], ry_recv.at[i % 3], y_peer)

    def kv_copy(i):
        by, half = slot(i)
        piece = kvbuf.at[by, half, core]
        return remote(piece, piece, kv_send.at[by, half], kv_recv.at[by, half], core_peer)

    def out_y_copy(i):
        piece = abuf.at[i % 3, core, ypos]
        return remote(piece, piece, ay_send.at[i % 3], ay_recv.at[i % 3], y_peer)

    def out_core_copy(i):
        piece = abuf.at[i % 3, core]
        return remote(piece, piece, ac_send.at[i % 3], ac_recv.at[i % 3], core_peer)

    def scatter_copy(i):
        by, half = slot(i)
        return remote(zsend.at[i % 2], zrecv.at[by - 1, half], zr_send.at[i % 2], zr_recv.at[by - 1, half], {"ty": flip(z, by)})

    loads = [pltpu.make_async_copy(w, w_in.at[n], w_sem.at[n]) for n, w in enumerate((wq_hbm, wk_hbm, wv_hbm))]
    loads.append(pltpu.make_async_copy(wo_hbm, w_out, w_sem.at[3]))
    for load in loads:
        load.start()
    greet(z, me)

    def send_own(half):
        @pl.when(z < 3)
        def _():
            to_right(half).start()

        @pl.when(z > 0)
        def _():
            to_left(half).start()

    norm_rows(x_ref, xall.at[0], stats, s_send, s_recv, core_peer, y_peer, send_own)
    for load in loads:
        load.wait()

    def step(i, carry):
        @pl.when(i < steps)
        def _():
            by, half = slot(i)
            first = (i >= 1) & (i <= 2)

            @pl.when(first & (z > 0))
            def _():
                arrived(left_slot, half)

            @pl.when(first & (z > 0) & (z < 3))
            def _():
                on_right(half).start()

            @pl.when(first & (z < 3))
            def _():
                arrived(right_slot, half)

            @pl.when(first & (z > 0) & (z < 3))
            def _():
                on_left(half).start()

            second = (i >= 3) & (i <= 4)

            @pl.when(second)
            def _():
                arrived(2, half)

            @pl.when(second & (z > 0) & (z < 3))
            def _():
                to_end(half).start()

            @pl.when((i >= 5) & (i <= 6) & (z != 1) & (z != 2))
            def _():
                arrived(3, half)

            def product(t, carry):
                part = jnp.dot(xall[by, half], w_in[t], preferred_element_type=F32).astype(BF)
                for side in range(2):
                    block = slice(side * piece_rows, (side + 1) * piece_rows)
                    pbuf[side, 0, t] = part[block, :half_cols]
                    pbuf[side, 1, t] = part[block, half_cols:]
                return carry

            lax.fori_loop(0, 3, product, 0)
            core_copy(i).start()
            core_copy(i).wait()

            def add(t, carry):
                for side in range(2):
                    sbuf[i % 2, side, t] = (pbuf[core, side, t].astype(F32) + r1[i % 2, side, t].astype(F32)).astype(BF)
                return carry

            lax.fori_loop(0, 3, add, 0)
            y_copy(i).start()

        @pl.when((i >= 1) & (i <= steps))
        def _():
            j = i - 1
            by, half = slot(j)
            y_copy(j).wait()
            for h in range(heads):
                cols = slice(h * HEAD_DIM, (h + 1) * HEAD_DIM)

                def total(n):
                    return (sbuf[j % 2, ypos, n, :, cols].astype(F32) + r2[j % 3, n, :, cols].astype(F32)).astype(BF)

                def turned(vals):
                    vals = vals.astype(F32)
                    return (vals * cos_ref[half, core] + pltpu.roll(vals, HEAD_DIM // 2, 1) * sin_ref[half, core]).astype(BF)

                qbuf[:, cols] = turned(total(0))
                kvbuf[by, half, core, 0, :, cols] = turned(total(1))
                kvbuf[by, half, core, 1, :, cols] = total(2)
            kv_copy(j).start()
            kv_copy(j).wait()

            def attend(n_halves):
                n_keys = n_halves * rows
                q_pos = (n_halves - 1) * rows + core * piece_rows + lax.broadcasted_iota(jnp.int32, (piece_rows, n_keys), 0)
                allowed = q_pos >= lax.broadcasted_iota(jnp.int32, (piece_rows, n_keys), 1)
                for h in range(heads):
                    cols = slice(h * HEAD_DIM, (h + 1) * HEAD_DIM)
                    keys = kvbuf[by, :n_halves, :, 0, :, cols].reshape(n_keys, HEAD_DIM)
                    vals = kvbuf[by, :n_halves, :, 1, :, cols].reshape(n_keys, HEAD_DIM)
                    scores = lax.dot_general(qbuf[:, cols], keys, (((1,), (1,)), ((), ())), preferred_element_type=F32) * HEAD_DIM ** -0.5
                    scores = jnp.where(allowed, scores, -1e30)
                    weight = jnp.exp(scores - jnp.max(scores, axis=1, keepdims=True))
                    prob = (weight / jnp.sum(weight, axis=1, keepdims=True)).astype(BF)
                    abuf[j % 3, core, ypos, :, cols] = jnp.dot(prob, vals, preferred_element_type=F32).astype(BF)

            @pl.when(half == 0)
            def _():
                attend(1)

            @pl.when(half == 1)
            def _():
                attend(2)

            out_y_copy(j).start()

        @pl.when(i >= 2)
        def _():
            j = i - 2
            by, half = slot(j)
            out_y_copy(j).wait()
            out_core_copy(j).start()

            @pl.when((j >= 3) & (j < steps - 1))
            def _():
                scatter_copy(j - 2).wait_send()

            out_core_copy(j).wait()

            def out(t, carry):
                cols = pl.ds(pl.multiple_of(t * 256, 256), 256)
                part = jnp.dot(abuf[j % 3, :, 0].reshape(rows, half_cols), w_out[0:half_cols, cols], preferred_element_type=F32)
                part += jnp.dot(abuf[j % 3, :, 1].reshape(rows, half_cols), w_out[half_cols:, cols], preferred_element_type=F32)

                @pl.when(by == 0)
                def _():
                    own[half, :, cols] = part

                @pl.when(by > 0)
                def _():
                    zsend[j % 2, :, cols] = part.astype(BF)
                return carry

            lax.fori_loop(0, width // 256, out, 0)

            @pl.when(by > 0)
            def _():
                scatter_copy(j).start()
        return carry

    lax.fori_loop(0, steps + 2, step, 0)

    for half in range(halves):
        @pl.when(z < 3)
        def _():
            to_right(half).wait_send()

        @pl.when(z > 0)
        def _():
            to_left(half).wait_send()

        @pl.when((z > 0) & (z < 3))
        def _():
            on_right(half).wait_send()
            on_left(half).wait_send()
            to_end(half).wait_send()

    for j in (steps - 3, steps - 2):
        scatter_copy(j).wait_send()
    for half in range(halves):
        for by in (1, 2, 3):
            remote(zsend.at[0], zrecv.at[by - 1, half], zr_send.at[0], zr_recv.at[by - 1, half], {"ty": flip(z, by)}).wait_recv()

        def finish(t, carry):
            part = pl.ds(pl.multiple_of(t * 32, 32), 32)
            total = own[half, part]
            for by in range(3):
                total += zrecv[by, half, part].astype(F32)
            out_ref[half, part] = (x_ref[half, part].astype(F32) + total.astype(BF).astype(F32)).astype(BF)
            return carry

        lax.fori_loop(0, rows // 32, finish, 0)


def attention(x, w_q, w_k, w_v, w_o):
    seq_len, width = x.shape
    rows, half_cols = seq_len // 2, width // 2
    piece_rows = rows // 2
    cos_t, sin_t = rot_tables(seq_len)
    dma, vmem = pltpu.SemaphoreType.DMA, pltpu.VMEM
    in_vmem, anywhere = pl.BlockSpec(memory_space=pltpu.VMEM), pl.BlockSpec(memory_space=pl.ANY)
    out = pl.pallas_call(
        attn_kernel,
        name="attention",
        out_shape=jax.ShapeDtypeStruct((2, rows, width), BF),
        in_specs=[in_vmem] * 3 + [anywhere] * 4,
        out_specs=in_vmem,
        scratch_shapes=[
            vmem((4, 2, rows, width), BF),
            vmem((3, width, width), BF),
            vmem((width, width), BF),
            vmem((2, 2, 3, piece_rows, half_cols), BF),
            vmem((2, 2, 3, piece_rows, half_cols), BF),
            vmem((2, 2, 3, piece_rows, half_cols), BF),
            vmem((3, 3, piece_rows, half_cols), BF),
            vmem((piece_rows, half_cols), BF),
            vmem((4, 2, 2, 2, piece_rows, half_cols), BF),
            vmem((3, 2, 2, piece_rows, half_cols), BF),
            vmem((2, rows, width), BF),
            vmem((3, 2, rows, width), BF),
            vmem((2, rows, width), F32),
            vmem((4, 8, seq_len), F32), dma((2,)), dma((2,)),
            dma((4,)), dma((5, 2)), dma((4, 2)),
            dma((2,)), dma((2,)), dma((3,)), dma((3,)), dma((4, 2)), dma((4, 2)),
            dma((3,)), dma((3,)), dma((3,)), dma((3,)),
            dma((2,)), dma((3, 2)),
        ],
        compiler_params=pltpu.CompilerParams(collective_id=1, has_side_effects=True, vmem_limit_bytes=VMEM_LIMIT),
    )(x.reshape(2, rows, width), jnp.asarray(cos_t).reshape(2, 2, piece_rows, HEAD_DIM), jnp.asarray(sin_t).reshape(2, 2, piece_rows, HEAD_DIM), w_q, w_k, w_v, w_o)
    return out.reshape(seq_len, width)


def mlp_kernel(h_ref, wg_hbm, wu_hbm, wd_hbm, out_ref, xall, w_in, w_out, pbuf, r1, sbuf, r2, abuf, zsend, zrecv, own,
               stats, s_send, s_recv, w_sem, az_send, az_recv, p_send, p_recv, ry_send, ry_recv, ay_send, ay_recv, ac_send, ac_recv, zr_send, zr_recv):
    z, me = lax.axis_index("ty"), lax.axis_index("tx")
    core, ypos = me % 2, me // 2
    core_peer, y_peer = {"tx": flip(me, 1)}, {"tx": flip(me, 2)}
    halves, rows, width = h_ref.shape
    ff = wg_hbm.shape[1]
    tiles = ff // TILE
    all_tiles = 2 * tiles
    quarter = rows // 4
    steps = 4 * halves
    pairs = ((0, (tiles + 1) // 2), ((tiles + 1) // 2, tiles))

    def slot(i):
        return ((i + 1) // 2) % 4, (i + 1) % 2

    right_slot, left_slot = 1 + 2 * (z % 2), 3 - 2 * (z % 2)

    def to_right(half):
        return remote(xall.at[0, half], xall.at[right_slot, half], az_send.at[0, half], az_recv.at[right_slot, half], {"ty": (z + 1) % 4})

    def to_left(half):
        return remote(xall.at[0, half], xall.at[left_slot, half], az_send.at[1, half], az_recv.at[left_slot, half], {"ty": (z + 3) % 4})

    def on_right(half):
        return remote(xall.at[left_slot, half], xall.at[2, half], az_send.at[2, half], az_recv.at[2, half], {"ty": (z + 1) % 4})

    def on_left(half):
        return remote(xall.at[right_slot, half], xall.at[2, half], az_send.at[3, half], az_recv.at[2, half], {"ty": (z + 3) % 4})

    def to_end(half):
        return remote(xall.at[2, half], xall.at[3, half], az_send.at[4, half], az_recv.at[3, half], {"ty": (3 * z + 1) % 4})

    def arrived(by, half):
        remote(xall.at[by, half], xall.at[by, half], az_send.at[0, half], az_recv.at[by, half], {"ty": flip(z, 1)}).wait_recv()

    def core_copy(i, part):
        group = pl.ds(2 * pairs[part][0], 2 * (pairs[part][1] - pairs[part][0]))
        return remote(pbuf.at[1 - core, group], r1.at[i % 2, group], p_send.at[i % 2, part], p_recv.at[i % 2, part], core_peer)

    def y_copy(i, part):
        group = pl.ds(2 * pairs[part][0], 2 * (pairs[part][1] - pairs[part][0]))
        return remote(sbuf.at[i % 2, 1 - ypos, group], r2.at[i % 3, group], ry_send.at[i % 3, part], ry_recv.at[i % 3, part], y_peer)

    def act_y_copy(i, part):
        cols = pl.ds(pairs[part][0] * TILE, (pairs[part][1] - pairs[part][0]) * TILE)
        piece = abuf.at[i % 3, core, ypos, :, cols]
        return remote(piece, piece, ay_send.at[i % 3, part], ay_recv.at[i % 3, part], y_peer)

    def act_core_copy(i):
        piece = abuf.at[i % 3, core]
        return remote(piece, piece, ac_send.at[i % 3], ac_recv.at[i % 3], core_peer)

    def scatter_copy(i):
        by, half = slot(i)
        return remote(zsend.at[i % 2], zrecv.at[by - 1, half], zr_send.at[i % 2], zr_recv.at[by - 1, half], {"ty": flip(z, by)})

    loads = [
        pltpu.make_async_copy(wg_hbm, w_in.at[:, pl.ds(0, ff)], w_sem.at[0]),
        pltpu.make_async_copy(wu_hbm, w_in.at[:, pl.ds(ff, ff)], w_sem.at[1]),
        pltpu.make_async_copy(wd_hbm, w_out, w_sem.at[2]),
    ]
    for load in loads:
        load.start()
    greet(z, me)

    def send_own(half):
        @pl.when(z < 3)
        def _():
            to_right(half).start()

        @pl.when(z > 0)
        def _():
            to_left(half).start()

    norm_rows(h_ref, xall.at[0], stats, s_send, s_recv, core_peer, y_peer, send_own)
    loads[0].wait()
    loads[1].wait()

    def step(i, carry):
        @pl.when(i < steps)
        def _():
            by, half = slot(i)

            first = (i >= 1) & (i <= 2)

            @pl.when(first & (z > 0))
            def _():
                arrived(left_slot, half)

            @pl.when(first & (z > 0) & (z < 3))
            def _():
                on_right(half).start()

            @pl.when(first & (z < 3))
            def _():
                arrived(right_slot, half)

            @pl.when(first & (z > 0) & (z < 3))
            def _():
                on_left(half).start()

            second = (i >= 3) & (i <= 4)

            @pl.when(second)
            def _():
                arrived(2, half)

            @pl.when(second & (z > 0) & (z < 3))
            def _():
                to_end(half).start()

            @pl.when((i >= 5) & (i <= 6) & (z != 1) & (z != 2))
            def _():
                arrived(3, half)

            def product(t, carry):
                for side in range(2):
                    cols = pl.ds(pl.multiple_of(side * ff + t * TILE, TILE), TILE)
                    part = jnp.dot(xall[by, half], w_in[:, cols], preferred_element_type=F32).astype(BF)
                    pbuf[:, 2 * t + side] = part.reshape(2, 2, quarter, TILE)
                return carry

            for part in range(2):
                lax.fori_loop(*pairs[part], product, 0)
                core_copy(i, part).start()
            for part in range(2):
                core_copy(i, part).wait_recv()

                def add(t, carry):
                    total = pbuf[core, t].astype(F32) + r1[i % 2, t].astype(F32)
                    total = total.astype(BF)
                    sbuf[i % 2, 0, t] = total[0]
                    sbuf[i % 2, 1, t] = total[1]
                    return carry

                lax.fori_loop(2 * pairs[part][0], 2 * pairs[part][1], add, 0)
                y_copy(i, part).start()
            for part in range(2):
                core_copy(i, part).wait_send()

        @pl.when((i >= 1) & (i <= steps))
        def _():
            j = i - 1

            def gate(t, carry):
                g = (sbuf[j % 2, ypos, 2 * t].astype(F32) + r2[j % 3, 2 * t].astype(F32)).astype(BF).astype(F32)
                u = (sbuf[j % 2, ypos, 2 * t + 1].astype(F32) + r2[j % 3, 2 * t + 1].astype(F32)).astype(BF).astype(F32)
                cols = pl.ds(pl.multiple_of(t * TILE, TILE), TILE)
                abuf[j % 3, core, ypos, :, cols] = (g * jax.nn.sigmoid(g) * u).astype(BF)
                return carry

            for part in range(2):
                y_copy(j, part).wait()
                lax.fori_loop(*pairs[part], gate, 0)
                act_y_copy(j, part).start()

        @pl.when(i >= 2)
        def _():
            j = i - 2
            by, half = slot(j)
            act_y_copy(j, 0).wait()
            act_y_copy(j, 1).wait()
            act_core_copy(j).start()

            @pl.when(j == 0)
            def _():
                loads[2].wait()

            @pl.when((j >= 3) & (j < steps - 1))
            def _():
                scatter_copy(j - 2).wait_send()

            act_core_copy(j).wait()

            def down(t, carry):
                cols = pl.ds(pl.multiple_of(t * 256, 256), 256)
                part = jnp.dot(abuf[j % 3].reshape(rows, ff), w_out[:, cols], preferred_element_type=F32)

                @pl.when(by == 0)
                def _():
                    own[half, :, cols] = part

                @pl.when(by > 0)
                def _():
                    zsend[j % 2, :, cols] = part.astype(BF)
                return carry

            lax.fori_loop(0, width // 256, down, 0)

            @pl.when(by > 0)
            def _():
                scatter_copy(j).start()
        return carry

    lax.fori_loop(0, steps + 2, step, 0)

    for half in range(halves):
        @pl.when(z < 3)
        def _():
            to_right(half).wait_send()

        @pl.when(z > 0)
        def _():
            to_left(half).wait_send()

        @pl.when((z > 0) & (z < 3))
        def _():
            on_right(half).wait_send()
            on_left(half).wait_send()
            to_end(half).wait_send()

    for j in (steps - 3, steps - 2):
        scatter_copy(j).wait_send()
    for half in range(halves):
        for by in (1, 2, 3):
            remote(zsend.at[0], zrecv.at[by - 1, half], zr_send.at[0], zr_recv.at[by - 1, half], {"ty": flip(z, by)}).wait_recv()

        def finish(t, carry):
            part = pl.ds(pl.multiple_of(t * 32, 32), 32)
            total = own[half, part]
            for by in range(3):
                total += zrecv[by, half, part].astype(F32)
            out_ref[half, part] = (h_ref[half, part].astype(F32) + total.astype(BF).astype(F32)).astype(BF)
            return carry

        lax.fori_loop(0, rows // 32, finish, 0)


def mlp(h, w_gate, w_up, w_down):
    seq_len, width = h.shape
    ff = w_gate.shape[1]
    halves = 2
    rows = seq_len // halves
    quarter = rows // 4
    tiles = ff // TILE
    dma, vmem = pltpu.SemaphoreType.DMA, pltpu.VMEM
    in_vmem, anywhere = pl.BlockSpec(memory_space=pltpu.VMEM), pl.BlockSpec(memory_space=pl.ANY)
    out = pl.pallas_call(
        mlp_kernel,
        name="mlp",
        out_shape=jax.ShapeDtypeStruct((halves, rows, width), BF),
        in_specs=[in_vmem, anywhere, anywhere, anywhere],
        out_specs=in_vmem,
        scratch_shapes=[
            vmem((4, halves, rows, width), BF),
            vmem((width, 2 * ff), BF),
            vmem((ff, width), BF),
            vmem((2, 2 * tiles, 2, quarter, TILE), BF),
            vmem((2, 2 * tiles, 2, quarter, TILE), BF),
            vmem((2, 2, 2 * tiles, quarter, TILE), BF),
            vmem((3, 2 * tiles, quarter, TILE), BF),
            vmem((3, 2, 2, quarter, ff), BF),
            vmem((2, rows, width), BF),
            vmem((3, halves, rows, width), BF),
            vmem((halves, rows, width), F32),
            vmem((4, 8, seq_len), F32), dma((2,)), dma((2,)),
            dma((3,)), dma((5, halves)), dma((4, halves)),
            dma((2, 2)), dma((2, 2)), dma((3, 2)), dma((3, 2)),
            dma((3, 2)), dma((3, 2)), dma((3,)), dma((3,)),
            dma((2,)), dma((3, halves)),
        ],
        compiler_params=pltpu.CompilerParams(collective_id=0, has_side_effects=True, vmem_limit_bytes=VMEM_LIMIT),
    )(h.reshape(halves, rows, width), w_gate, w_up, w_down)
    return out.reshape(seq_len, width)


def solution(mesh):
    act_spec = P(("dp", "ty"), None, "tx")
    col_spec = P("tx", "ty")
    row_spec = P("ty", "tx")

    def layer_fn(x_blk, w_q, w_k, w_v, w_o, w_gate, w_up, w_down):
        h = attention(x_blk[0], w_q, w_k, w_v, w_o)
        return mlp(h, w_gate, w_up, w_down)[None]

    return jax.shard_map(layer_fn, mesh=mesh, in_specs=(act_spec, col_spec, col_spec, col_spec, row_spec, col_spec, col_spec, row_spec), out_specs=act_spec, check_vma=False)
```

time: 518 us -> 488 us (0.942)
  the two profiles are of different devices: /device:TPU:0 before, /device:TPU:10 now
where the time goes in v2:
time: 488 us
  Pallas kernels  485 us (99%)
    pallas_call x1, Pallas kernels, mlp(): pl.pallas_call(mlp_kernel, name='mlp', out_shape=jax.ShapeDtypeStruct((ha...  275 us
    pallas_call x1, Pallas kernels, attention(): pl.pallas_call(attn_kernel, name='attention', out_shape=jax.ShapeDtypeStr...  211 us

profile of v2, /device:TPU:10, one launch (start us, length us, event | category | flops | bytes accessed | tf_op | source)
XLA Modules:
  0.0 487.9 jit_solution(9676444450242991767)
XLA Ops:
  0.0 210.6 %attention.1.h_ref = bf16[2,256,1280]{2,1,0:T(8,128)(2,1)} custom-call(bf16[2,256,1280]{2,1,0:T(8,128)(2,1)} %bitcast.3, f32[2,2,128,128]{3,2,1,0:T(8,128)} %constant.7.cos_ref, f32[2,2,128,128]{3,2,1,0:T(8,128)} %constant.8.sin_ref, bf16[1280,1280]{1,0:T(8,128)(2,1)} %wq_hbm.1, bf16[1280,1280]{1,0:T(8,128)(2,1)} %wk_hbm.1, bf16[1280,1280]{1,0:T(8,128)(2,1)} %wv_hbm.1, ...), custom_call_target="tpu_custom_call" | custom-call | tf_op jit(solution)/shard_map/attention/pallas_call | solution.py:330
  210.6 274.8 %mlp.1 = bf16[2,256,1280]{2,1,0:T(8,128)(2,1)} custom-call(bf16[2,256,1280]{2,1,0:T(8,128)(2,1)} %attention.1.h_ref, bf16[1280,3456]{1,0:T(8,128)(2,1)} %wg_hbm.1, bf16[1280,3456]{1,0:T(8,128)(2,1)} %wu_hbm.1, bf16[3456,1280]{1,0:T(8,128)(2,1)} %wd_hbm.1), custom_call_target="tpu_custom_call" | custom-call | tf_op jit(solution)/shard_map/mlp/pallas_call | solution.py:599
  485.4 2.5 copy.12

commit v3 on v2

--- a/solution.py
+++ b/solution.py
@@ -72,8 +72,8 @@
     return pltpu.make_async_remote_copy(src_ref=src, dst_ref=dst, send_sem=send_sem, recv_sem=recv_sem, device_id=device_id, device_id_type=MESH)
 
 
-def attn_kernel(x_ref, cos_ref, sin_ref, wq_hbm, wk_hbm, wv_hbm, wo_hbm, out_ref, xall, w_in, w_out, pbuf, r1, sbuf, r2, qbuf, kvbuf, abuf, zsend, zrecv, own,
-                stats, s_send, s_recv, w_sem, az_send, az_recv, p_send, p_recv, ry_send, ry_recv, kv_send, kv_recv, ay_send, ay_recv, ac_send, ac_recv, zr_send, zr_recv):
+def attn_kernel(x_ref, cos_ref, sin_ref, wq_hbm, wk_hbm, wv_hbm, wo_hbm, out_ref, xall, w_in, w_out, pbuf, r1, sbuf, r2, qbuf, kvbuf, abuf, zsend, zrecv, cbuf, rbuf, own,
+                stats, s_send, s_recv, w_sem, az_send, az_recv, p_send, p_recv, ry_send, ry_recv, kv_send, kv_recv, ay_send, ay_recv, ac_send, ac_recv, zr_send, zr_recv, rl_recv, cb_send):
     z, me = lax.axis_index("ty"), lax.axis_index("tx")
     core, ypos = me % 2, me // 2
     core_peer, y_peer = {"tx": flip(me, 1)}, {"tx": flip(me, 2)}
@@ -128,9 +128,27 @@
         piece = abuf.at[i % 3, core]
         return remote(piece, piece, ac_send.at[i % 3], ac_recv.at[i % 3], core_peer)
 
-    def scatter_copy(i):
-        by, half = slot(i)
-        return remote(zsend.at[i % 2], zrecv.at[by - 1, half], zr_send.at[i % 2], zr_recv.at[by - 1, half], {"ty": flip(z, by)})
+    def direct_copy(i):
+        half = slot(i)[1]
+        return remote(zsend.at[i % 2], zrecv.at[0, half], zr_send.at[i % 2], zr_recv.at[0, half], {"ty": flip(z, 1)})
+
+    def relay_copy(i):
+        half, far = slot(i)[1], ((i + 1) // 2) % 2
+        return remote(zsend.at[i % 2], rbuf.at[far, half], zr_send.at[i % 2], rl_recv.at[far, half], {"ty": flip(z, 1)})
+
+    def cross_copy(far, half):
+        return remote(cbuf.at[far, half], zrecv.at[1, half], cb_send.at[far, half], zr_recv.at[1, half], {"ty": flip(z, 3 - far)})
+
+    def combine(far, half):
+        remote(cbuf.at[far, half], rbuf.at[far, half], cb_send.at[far, half], rl_recv.at[far, half], {"ty": flip(z, 1)}).wait_recv()
+
+        def add(t, carry):
+            part = pl.ds(pl.multiple_of(t * 32, 32), 32)
+            cbuf[far, half, part] = (cbuf[far, half, part].astype(F32) + rbuf[far, half, part].astype(F32)).astype(BF)
+            return carry
+
+        lax.fori_loop(0, rows // 32, add, 0)
+        cross_copy(far, half).start()
 
     loads = [pltpu.make_async_copy(w, w_in.at[n], w_sem.at[n]) for n, w in enumerate((wq_hbm, wk_hbm, wv_hbm))]
     loads.append(pltpu.make_async_copy(wo_hbm, w_out, w_sem.at[3]))
@@ -259,9 +277,9 @@
             out_y_copy(j).wait()
             out_core_copy(j).start()
 
-            @pl.when((j >= 3) & (j < steps - 1))
-            def _():
-                scatter_copy(j - 2).wait_send()
+            @pl.when((inner == 0) & (j >= 3) & (j < steps - 1))
+            def _():
+                direct_copy(j - 2).wait_send()
 
             out_core_copy(j).wait()
 
@@ -274,16 +292,32 @@
                 def _():
                     own[half, :, cols] = part
 
-                @pl.when(by > 0)
+                @pl.when((by > 0) & ((inner == 0) | (j > 4)))
                 def _():
                     zsend[j % 2, :, cols] = part.astype(BF)
+
+                @pl.when((by > 0) & (inner == 1) & (j <= 4))
+                def _():
+                    cbuf[((j + 1) // 2 + 1) % 2, half, :, cols] = part.astype(BF)
                 return carry
 
             lax.fori_loop(0, width // 256, out, 0)
 
-            @pl.when(by > 0)
-            def _():
-                scatter_copy(j).start()
+            @pl.when(((inner == 0) & (j >= 1) & (j <= 2)) | ((inner == 1) & (j >= 5) & (j <= 6)))
+            def _():
+                direct_copy(j).start()
+
+            @pl.when((inner == 0) & (j >= 3) & (j <= 6))
+            def _():
+                relay_copy(j).start()
+
+        @pl.when((inner == 1) & (i == steps - 1))
+        def _():
+            combine(0, 0)
+
+        @pl.when((inner == 1) & (i == steps))
+        def _():
+            combine(0, 1)
         return carry
 
     lax.fori_loop(0, steps + 2, step, 0)
@@ -303,17 +337,27 @@
             on_left(half).wait_send()
             to_end(half).wait_send()
 
+    @pl.when(inner == 1)
+    def _():
+        combine(1, 0)
+        combine(1, 1)
+
     for j in (steps - 3, steps - 2):
-        scatter_copy(j).wait_send()
+        direct_copy(j).wait_send()
     for half in range(halves):
-        for by in (1, 2, 3):
-            remote(zsend.at[0], zrecv.at[by - 1, half], zr_send.at[0], zr_recv.at[by - 1, half], {"ty": flip(z, by)}).wait_recv()
+        @pl.when(inner == 1)
+        def _():
+            cross_copy(0, half).wait_send()
+            cross_copy(1, half).wait_send()
+
+        for source in range(2):
+            remote(zsend.at[0], zrecv.at[source, half], zr_send.at[0], zr_recv.at[source, half], {"ty": flip(z, 1)}).wait_recv()
 
         def finish(t, carry):
             part = pl.ds(pl.multiple_of(t * 32, 32), 32)
             total = own[half, part]
-            for by in range(3):
-                total += zrecv[by, half, part].astype(F32)
+            for source in range(2):
+                total += zrecv[source, half, part].astype(F32)
             out_ref[half, part] = (x_ref[half, part].astype(F32) + total.astype(BF).astype(F32)).astype(BF)
             return carry
 
@@ -345,13 +389,15 @@
             vmem((4, 2, 2, 2, piece_rows, half_cols), BF),
             vmem((3, 2, 2, piece_rows, half_cols), BF),
             vmem((2, rows, width), BF),
-            vmem((3, 2, rows, width), BF),
+            vmem((2, 2, rows, width), BF),
+            vmem((2, 2, rows, width), BF),
+            vmem((2, 2, rows, width), BF),
             vmem((2, rows, width), F32),
             vmem((4, 8, seq_len), F32), dma((2,)), dma((2,)),
             dma((4,)), dma((5, 2)), dma((4, 2)),
             dma((2,)), dma((2,)), dma((3,)), dma((3,)), dma((4, 2)), dma((4, 2)),
             dma((3,)), dma((3,)), dma((3,)), dma((3,)),
-            dma((2,)), dma((3, 2)),
+            dma((2,)), dma((2, 2)), dma((2, 2)), dma((2, 2)),
         ],
         compiler_params=pltpu.CompilerParams(collective_id=1, has_side_effects=True, vmem_limit_bytes=VMEM_LIMIT),
     )(x.reshape(2, rows, width), jnp.asarray(cos_t).reshape(2, 2, piece_rows, HEAD_DIM), jnp.asarray(sin_t).reshape(2, 2, piece_rows, HEAD_DIM), w_q, w_k, w_v, w_o)

time: 488 us -> 458 us (0.939)
  the two profiles are of different devices: /device:TPU:10 before, /device:TPU:12 now
where the time goes in v3:
time: 458 us
  Pallas kernels  456 us (100%)
    pallas_call x1, Pallas kernels, mlp(): pl.pallas_call(mlp_kernel, name='mlp', out_shape=jax.ShapeDtypeStruct((ha...  275 us
    pallas_call x1, Pallas kernels, attention(): pl.pallas_call(attn_kernel, name='attention', out_shape=jax.ShapeDtypeStr...  181 us

profile of v3, /device:TPU:12, one launch (start us, length us, event | category | flops | bytes accessed | tf_op | source)
XLA Modules:
  0.0 458.3 jit_solution(1300412972360445758)
XLA Ops:
  0.0 180.6 %attention.1.h_ref = bf16[2,256,1280]{2,1,0:T(8,128)(2,1)} custom-call(bf16[2,256,1280]{2,1,0:T(8,128)(2,1)} %bitcast.3, f32[2,2,128,128]{3,2,1,0:T(8,128)} %constant.7.cos_ref, f32[2,2,128,128]{3,2,1,0:T(8,128)} %constant.8.sin_ref, bf16[1280,1280]{1,0:T(8,128)(2,1)} %wq_hbm.1, bf16[1280,1280]{1,0:T(8,128)(2,1)} %wk_hbm.1, bf16[1280,1280]{1,0:T(8,128)(2,1)} %wv_hbm.1, ...), custom_call_target="tpu_custom_call" | custom-call | tf_op jit(solution)/shard_map/attention/pallas_call | solution.py:374
  180.6 275.3 %mlp.1 = bf16[2,256,1280]{2,1,0:T(8,128)(2,1)} custom-call(bf16[2,256,1280]{2,1,0:T(8,128)(2,1)} %attention.1.h_ref, bf16[1280,3456]{1,0:T(8,128)(2,1)} %wg_hbm.1, bf16[1280,3456]{1,0:T(8,128)(2,1)} %wu_hbm.1, bf16[3456,1280]{1,0:T(8,128)(2,1)} %wd_hbm.1), custom_call_target="tpu_custom_call" | custom-call | tf_op jit(solution)/shard_map/mlp/pallas_call | solution.py:645
  455.8 2.5 copy.12
